TPU v7x, 256 devices: a whole 4x4x8 slice. The times are simulated.
256 devices in a mesh: row: 8 (over y, core), col: 32 (over x, z).
Axes of the slice: x: 4, y: 4, z: 8, core: 2. Of those that a mesh axis runs over, the one named last changes fastest.
Arguments:
- phases: int32 [8, 32, 8, 24, 576], P('row', 'col'), may hold values from 0 to 2
- grain: float32 [8, 32, 8, 24, 576], P('row', 'col'), may hold values from 0.5 to 2
- phase_cond: float32 [3], replicated, may hold values from 0.3 to 3
- micro_counts: int32 [8, 32, 8], P('row', 'col'), may hold values from 6 to 12, as said below
- current: float32 [8, 32, 8], P('row', 'col'), may hold values from -5 to 5
- load: float32 [8, 32, 8], P('row', 'col'), may hold values from -16 to 16
Outputs:
- states: float32 [8, 32, 8, 3, 24, 576], P('row', 'col')
- tangent: float32 [8, 32, 8, 3, 3], P('row', 'col')
- increment: float32 [8, 32, 8], P('row', 'col')
- residual: float32 [8, 32, 8], P('row', 'col')
Inputs may be any that keep to these rules, and one draw needn't show every extreme that they name: `micro_counts`: every draw has an element with 12 inner iterations and one with 6.
All inputs are finite; a program needn't handle non-finite values.
Results may differ from a plain program's by a relative error of at most 0.0003.
Values sent between devices are 32-bit elements; how exact they have to be, the bound alone decides.
No kernel may reach another device: no remote copies, remote signals or barrier semaphores. Data moves between devices by JAX's collectives and lax.ppermute only.
A program may use at most 64 MiB of HBM per device.

v0:
```python
import jax
import jax.numpy as jnp
from jax import lax
from jax.sharding import Mesh
from jax.sharding import PartitionSpec as P

VOX = 24
YZ = 576
PHASES = 3
MACRO_ITERS = 8
ROW_COL = ("row_0", "row_1", "col_0", "col_1")
ROW = ("row_0", "row_1")
COL = ("col_0", "col_1")


def laid_out(pieces, dim):
    pieces = jnp.moveaxis(pieces, 0, dim)
    shape = pieces.shape
    return pieces.reshape(*shape[:dim], shape[dim] * shape[dim + 1], *shape[dim + 2 :])


def gather_in_order(shard, axes, turns):
    pieces = shard
    for k in turns:
        pieces = lax.all_gather(pieces, axes[k])
    done = turns[::-1]
    back = [done.index(k) for k in range(len(axes))]
    pieces = pieces.transpose(*back, *range(len(axes), pieces.ndim))
    return pieces.reshape(-1, *shard.shape)


def whole_of(shard, axes, turns, dim):
    return laid_out(gather_in_order(shard, axes, turns), dim)


def forward(field, axis_id):
    z_index = jnp.arange(YZ) % VOX
    if axis_id == 0:
        return jnp.roll(field, -1, axis=-2)
    if axis_id == 1:
        return jnp.roll(field, -VOX, axis=-1)
    return jnp.where(
        z_index == VOX - 1, jnp.roll(field, VOX - 1, axis=-1), jnp.roll(field, -1, axis=-1)
    )


def behind(field, axis_id):
    z_index = jnp.arange(YZ) % VOX
    if axis_id == 0:
        return jnp.roll(field, 1, axis=-2)
    if axis_id == 1:
        return jnp.roll(field, VOX, axis=-1)
    return jnp.where(z_index == 0, jnp.roll(field, 1 - VOX, axis=-1), jnp.roll(field, 1, axis=-1))


def solve_rve(conduct, count):
    faces = [(conduct + forward(conduct, axis_id)) * 0.5 for axis_id in range(3)]
    back_faces = [behind(faces[axis_id], axis_id) for axis_id in range(3)]
    rhs = jnp.stack([faces[axis_id] - back_faces[axis_id] for axis_id in range(3)])

    def operate(field):
        total = jnp.zeros_like(field)
        for axis_id in range(3):
            total = total + faces[axis_id] * (field - forward(field, axis_id))
            total = total + back_faces[axis_id] * (field - behind(field, axis_id))
        return total

    def sweep(index, carry):
        fluct, remain, direction, norm_now = carry
        image = operate(direction)
        step_size = norm_now / jnp.sum(direction * image, axis=(1, 2))
        fluct = fluct + step_size[:, None, None] * direction
        remain = remain - step_size[:, None, None] * image
        norm_next = jnp.sum(remain * remain, axis=(1, 2))
        direction = remain + (norm_next / norm_now)[:, None, None] * direction
        return (fluct, remain, direction, norm_next)

    start = (jnp.zeros_like(rhs), rhs, rhs, jnp.sum(rhs * rhs, axis=(1, 2)))
    fluct = lax.fori_loop(0, count, sweep, start)[0]
    identity = jnp.eye(3, dtype=conduct.dtype)
    rows_out = []
    for axis_id in range(3):
        flux = faces[axis_id][None] * (
            identity[axis_id][:, None, None] + forward(fluct, axis_id) - fluct
        )
        rows_out.append(jnp.mean(flux, axis=(1, 2)))
    return (fluct, jnp.stack(rows_out))


def solve_batch(conduct, counts):
    return lax.map(lambda pair: solve_rve(pair[0], pair[1]), (conduct, counts))


def neighbour(padded, axis_id, offset):
    lead = padded.ndim - 3
    index = [slice(None)] * lead + [slice(1, -1)] * 3
    length = padded.shape[lead + axis_id]
    index[lead + axis_id] = slice(1 + offset, length - 1 + offset)
    return padded[tuple(index)]


def coarse_apply(k_padded, v_padded):
    centre = neighbour(v_padded, 0, 0)
    total = jnp.zeros_like(centre)
    for axis_id in range(3):
        k_centre = neighbour(k_padded[axis_id], 0, 0)
        for offset in (1, -1):
            cond_face = 0.5 * (k_centre + neighbour(k_padded[axis_id], axis_id, offset))
            total = total + cond_face * (centre - neighbour(v_padded, axis_id, offset))
    return total


def coarse_cg(k_padded, residual, pad_field, norm_of, curv_of):
    increment = jnp.zeros_like(residual)
    direction = residual
    norm_now = norm_of(residual)
    for iteration in range(MACRO_ITERS):
        image = coarse_apply(k_padded, pad_field(direction))
        step_size = norm_now / curv_of(direction, image)
        increment = increment + step_size * direction
        residual = residual - step_size * image
        norm_next = norm_of(residual)
        direction = residual + norm_next / norm_now * direction
        norm_now = norm_next
    return (increment, residual)


def local_norm(field):
    return jnp.sum(field * field)


def local_curv(first, second):
    return jnp.sum(first * second)


def shards(phases, grain, phase_cond, micro_counts, current, load):
    depth = phases.shape[2]
    conduct = jnp.zeros(grain.shape, grain.dtype)
    for phase_id in range(PHASES):
        conduct = conduct + jnp.where(phases == phase_id, phase_cond[phase_id], 0.0)
    conduct = conduct * grain
    flat = conduct.reshape(depth, VOX, YZ)
    counts = micro_counts.reshape(depth)
    fluct, tangent = solve_batch(flat, counts)
    states = fluct.reshape(1, 1, depth, 3, VOX, YZ)
    tangent_out = tangent.reshape(1, 1, depth, 3, 3)
    diag = jnp.stack([tangent[:, axis_id, axis_id] for axis_id in range(3)]).reshape(3, 1, 1, depth)
    packed = jnp.concatenate(
        [diag, current.reshape(1, 1, 1, depth), load.reshape(1, 1, 1, depth)], axis=0
    ).reshape(5, 1, depth)
    whole = whole_of(packed, ROW_COL, (0, 2, 3, 1), 1)
    whole = whole.reshape(5, lax.axis_size(ROW), lax.axis_size(COL), depth)
    padded = jnp.pad(whole, ((0, 0), (1, 1), (1, 1), (1, 1)))
    residual = whole[4] - coarse_apply(padded[:3], padded[3])
    increment, residual = coarse_cg(
        padded[:3], residual, lambda field: jnp.pad(field, 1), local_norm, local_curv
    )
    row_at = lax.axis_index(ROW)
    col_at = lax.axis_index(COL)
    zero_at = jnp.zeros((), jnp.int32)
    increment = lax.dynamic_slice(increment, (row_at, col_at, zero_at), (1, 1, depth))
    residual = lax.dynamic_slice(residual, (row_at, col_at, zero_at), (1, 1, depth))
    return (states, tangent_out, increment, residual)


def solution(mesh):
    torus = Mesh(mesh.devices.reshape(4, 2, 4, 8), ("row_0", "row_1", "col_0", "col_1"))
    in_specs = (
        P(ROW, COL, None, None, None),
        P(ROW, COL, None, None, None),
        P(),
        P(ROW, COL, None),
        P(ROW, COL, None),
        P(ROW, COL, None),
    )
    out_specs = (
        P(ROW, COL, None, None, None, None),
        P(ROW, COL, None, None, None),
        P(ROW, COL, None),
        P(ROW, COL, None),
    )
    return jax.shard_map(
        shards, mesh=torus, in_specs=in_specs, out_specs=out_specs, check_vma=False
    )
```

profile of v0, /device:TPU:1, one launch (start us, length us, event | category | flops | bytes accessed | tf_op | source)
XLA Modules:
  0.0 322.9 jit_solution(15595284607173324453)
XLA Ops:
  0.6 1.4 fusion.241
  2.0 3.3 %multiply_bitcast_fusion.3 = f32[8,24,576]{2,1,0:T(8,128)S(1)} fusion(f32[1,1,8,24,576]{4,3,2,1,0:T(8,128)} %param.11, s32[1,1,8,24,576]{4,3,2,1,0:T(8,128)} %param.10, f32[]{:T(128)} %bitcast.31, f32[]{:T(128)} %bitcast.30, f32[]{:T(128)} %bitcast.29), kind=kLoop, calls=%fused_computation.108 | loop fusion | flops 995328 | bytes 1327116 | tf_op jit(solution)/shard_map/reshape | solution.py:142
  5.3 190.4 %while.43 = (s32[]{:T(128)}, f32[8,3,24,576]{3,2,1,0:T(8,128)S(1)}, f32[8,3,3]{2,1,0:T(4,128)S(1)}, f32[8,24,576]{2,1,0:T(8,128)S(1)}, s32[8]{0:T(128)S(1)}, /*i...) while((s32[]{:T(128)}, f32[8,3,24,576]{3,2,1,0:T(8,128)S(1)}, f32[8,3,3]{2,1,0:T(4,128)S(1)}, ...), condition=%wide.region_9.10_spmd, body=%wide.region_0.9_spmd.sunk | while | flops 2898470 | bytes 12391870 | solution.py:91
  6.7 0.6 dynamic_slice.81
  7.3 20.0 %while.44 = (s32[]{:T(128)}, f32[3,24,576]{2,1,0:T(8,128)S(1)}, f32[3,24,576]{2,1,0:T(8,128)S(1)}, f32[3,24,576]{2,1,0:T(8,128)S(1)}, f32[3]{0:T(128)S(1)}, /*in...) while((s32[]{:T(128)}, f32[3,24,576]{2,1,0:T(8,128)S(1)}, ...), condition=%wide.region_5.5_spmd, body=%wide.region_2.4_spmd.sunk | while | flops 1539074 | bytes 5974553 | solution.py:79
  8.6 0.4 multiply_reduce_fusion.23
  10.8 0.4 multiply_reduce_fusion.23
  12.9 0.4 multiply_reduce_fusion.23
  15.1 0.4 multiply_reduce_fusion.23
  17.2 0.4 multiply_reduce_fusion.23
  19.4 0.4 multiply_reduce_fusion.23
  29.4 0.6 dynamic_slice.81
  30.0 20.0 %while.44 = (s32[]{:T(128)}, f32[3,24,576]{2,1,0:T(8,128)S(1)}, f32[3,24,576]{2,1,0:T(8,128)S(1)}, f32[3,24,576]{2,1,0:T(8,128)S(1)}, f32[3]{0:T(128)S(1)}, /*in...) while((s32[]{:T(128)}, f32[3,24,576]{2,1,0:T(8,128)S(1)}, ...), condition=%wide.region_5.5_spmd, body=%wide.region_2.4_spmd.sunk | while | flops 1539074 | bytes 5974553 | solution.py:79
  31.4 0.4 multiply_reduce_fusion.23
  42.1 0.4 multiply_reduce_fusion.23
  52.2 0.6 dynamic_slice.81
  52.8 22.1 %while.44 = (s32[]{:T(128)}, f32[3,24,576]{2,1,0:T(8,128)S(1)}, f32[3,24,576]{2,1,0:T(8,128)S(1)}, f32[3,24,576]{2,1,0:T(8,128)S(1)}, f32[3]{0:T(128)S(1)}, /*in...) while((s32[]{:T(128)}, f32[3,24,576]{2,1,0:T(8,128)S(1)}, ...), condition=%wide.region_5.5_spmd, body=%wide.region_2.4_spmd.sunk | while | flops 1539074 | bytes 5974553 | solution.py:79
  54.1 0.4 multiply_reduce_fusion.23
  64.8 0.4 multiply_reduce_fusion.23
  77.0 0.6 dynamic_slice.81
  77.7 22.1 %while.44 = (s32[]{:T(128)}, f32[3,24,576]{2,1,0:T(8,128)S(1)}, f32[3,24,576]{2,1,0:T(8,128)S(1)}, f32[3,24,576]{2,1,0:T(8,128)S(1)}, f32[3]{0:T(128)S(1)}, /*in...) while((s32[]{:T(128)}, f32[3,24,576]{2,1,0:T(8,128)S(1)}, ...), condition=%wide.region_5.5_spmd, body=%wide.region_2.4_spmd.sunk | while | flops 1539074 | bytes 5974553 | solution.py:79
  81.1 0.4 multiply_reduce_fusion.23
  91.9 0.4 multiply_reduce_fusion.23
  101.9 0.6 dynamic_slice.81
  102.5 22.1 %while.44 = (s32[]{:T(128)}, f32[3,24,576]{2,1,0:T(8,128)S(1)}, f32[3,24,576]{2,1,0:T(8,128)S(1)}, f32[3,24,576]{2,1,0:T(8,128)S(1)}, f32[3]{0:T(128)S(1)}, /*in...) while((s32[]{:T(128)}, f32[3,24,576]{2,1,0:T(8,128)S(1)}, ...), condition=%wide.region_5.5_spmd, body=%wide.region_2.4_spmd.sunk | while | flops 1539074 | bytes 5974553 | solution.py:79
  110.3 0.4 multiply_reduce_fusion.23
  121.0 0.4 multiply_reduce_fusion.23
  126.8 0.6 dynamic_slice.81
  127.4 22.1 %while.44 = (s32[]{:T(128)}, f32[3,24,576]{2,1,0:T(8,128)S(1)}, f32[3,24,576]{2,1,0:T(8,128)S(1)}, f32[3,24,576]{2,1,0:T(8,128)S(1)}, f32[3]{0:T(128)S(1)}, /*in...) while((s32[]{:T(128)}, f32[3,24,576]{2,1,0:T(8,128)S(1)}, ...), condition=%wide.region_5.5_spmd, body=%wide.region_2.4_spmd.sunk | while | flops 1539074 | bytes 5974553 | solution.py:79
  135.2 0.4 multiply_reduce_fusion.23
  143.8 0.4 multiply_reduce_fusion.23
  151.7 0.6 dynamic_slice.81
  152.3 20.0 %while.44 = (s32[]{:T(128)}, f32[3,24,576]{2,1,0:T(8,128)S(1)}, f32[3,24,576]{2,1,0:T(8,128)S(1)}, f32[3,24,576]{2,1,0:T(8,128)S(1)}, f32[3]{0:T(128)S(1)}, /*in...) while((s32[]{:T(128)}, f32[3,24,576]{2,1,0:T(8,128)S(1)}, ...), condition=%wide.region_5.5_spmd, body=%wide.region_2.4_spmd.sunk | while | flops 1539074 | bytes 5974553 | solution.py:79
  157.9 0.4 multiply_reduce_fusion.23
  168.6 0.4 multiply_reduce_fusion.23
  174.4 0.6 dynamic_slice.81
  175.0 20.0 %while.44 = (s32[]{:T(128)}, f32[3,24,576]{2,1,0:T(8,128)S(1)}, f32[3,24,576]{2,1,0:T(8,128)S(1)}, f32[3,24,576]{2,1,0:T(8,128)S(1)}, f32[3]{0:T(128)S(1)}, /*in...) while((s32[]{:T(128)}, f32[3,24,576]{2,1,0:T(8,128)S(1)}, ...), condition=%wide.region_5.5_spmd, body=%wide.region_2.4_spmd.sunk | while | flops 1539074 | bytes 5974553 | solution.py:79
  184.9 0.4 multiply_reduce_fusion.23
  193.5 0.4 multiply_reduce_fusion.23
  196.0 44.6 %all-gather = f32[20,1,1,8]{3,2,1,0:T(1,128)S(1)} all-gather(f32[5,1,1,8]{3,2,1,0:T(1,128)S(1)} %copy.64), channel_id=2, replica_groups=mesh['row_0'=4,'row_1'=2,'col_0'=4,'col_1'=8] {'row_0'}, dimensions={0}, use_global_device_ids=true | all-gather | bytes 800 | tf_op jit(solution)/shard_map/all_gather | solution.py:25
  240.7 9.1 %all-gather.1 = f32[16,5,1,8]{3,2,1,0:T(1,128)S(1)} all-gather(f32[4,5,1,8]{3,2,1,0:T(1,128)S(1)} %bitcast.148), channel_id=3, replica_groups=mesh['row_0'=4,'row_1'=2,'col_0'=4,'col_1'=8] {'col_0'}, dimensions={0}, use_global_device_ids=true | all-gather | bytes 3200 | tf_op jit(solution)/shard_map/all_gather | solution.py:25
  249.8 28.6 %all-gather.2 = f32[32,4,5,1,8]{4,1,3,2,0:T(4,128)S(1)} all-gather(f32[4,4,5,1,8]{4,1,3,2,0:T(4,128)S(1)} %copy.65), channel_id=4, replica_groups=mesh['row_0'=4,'row_1'=2,'col_0'=4,'col_1'=8] {'col_1'}, dimensions={0}, use_global_device_ids=true | all-gather | bytes 23040 | tf_op jit(solution)/shard_map/all_gather | solution.py:25
  278.5 10.3 %all-gather.3 = f32[16,4,4,5,1,8]{5,1,0,3,2,4:T(4,128)S(1)} all-gather(f32[8,4,4,5,1,8]{5,1,0,3,2,4:T(4,128)S(1)} %bitcast.143), channel_id=5, replica_groups=mesh['row_0'=4,'row_1'=2,'col_0'=4,'col_1'=8] {'row_1'}, dimensions={0}, use_global_device_ids=true | all-gather | bytes 61440 | tf_op jit(solution)/shard_map/all_gather | solution.py:25
  288.8 0.5 copy.76
  289.2 0.4 copy.68
  289.7 0.7 reshape.338
  290.9 0.7 multiply_reduce_fusion.17
  292.9 0.6 multiply_reduce_fusion.16
  294.9 0.7 multiply_reduce_fusion.15
  296.9 0.6 multiply_reduce_fusion.14
  298.9 0.7 multiply_reduce_fusion.13
  300.9 0.6 multiply_reduce_fusion.12
  302.9 0.7 multiply_reduce_fusion.11
  304.9 0.6 multiply_reduce_fusion.10
  306.9 0.7 multiply_reduce_fusion.9
  308.9 0.6 multiply_reduce_fusion.8
  310.9 0.7 multiply_reduce_fusion.7
  312.9 0.6 multiply_reduce_fusion.6
  314.9 0.7 multiply_reduce_fusion.5
  316.9 0.6 multiply_reduce_fusion.4
  318.9 0.7 multiply_reduce_fusion.3
  321.0 0.6 copy.72
  321.6 0.6 copy.73
  322.2 0.7 copy.71
  (1502 shorter events, 115.8 us)
Async XLA Ops:
  0.6 4.7 %copy-start.3 = (s32[1,1,8]{2,1,0:T(1,128)S(1)}, s32[1,1,8]{2,1,0:T(1,128)}, u32[]{:S(2)}) copy-start(s32[1,1,8]{2,1,0:T(1,128)} %param.13) | copy-start | bytes 100
  5.3 190.7 %copy-start = (f32[1,1,8]{2,1,0:T(1,128)S(1)}, f32[1,1,8]{2,1,0:T(1,128)}, u32[]{:S(2)}) copy-start(f32[1,1,8]{2,1,0:T(1,128)} %param.15) | copy-start | bytes 100
  5.3 190.7 %copy-start.1 = (f32[1,1,8]{2,1,0:T(1,128)S(1)}, f32[1,1,8]{2,1,0:T(1,128)}, u32[]{:S(2)}) copy-start(f32[1,1,8]{2,1,0:T(1,128)} %param.14) | copy-start | bytes 100
  195.7 93.5 %copy-start.2 = (f32[8,3,24,576]{3,2,1,0:T(8,128)}, f32[8,3,24,576]{3,2,1,0:T(8,128)S(1)}, u32[]{:S(2)}) copy-start(f32[8,3,24,576]{3,2,1,0:T(8,128)S(1)} %get-tuple-element.269) | copy-start | bytes 3981316
where the time goes:
time: 327 us; the launch traced here: 323 us
  blocking collectives  92.7 us (28%)
  other arithmetic  83.2 us (25%)
  local copies, waits for them, and re-layouts  63.7 us (19%)
  loops' own time  62.4 us (19%)
  between operations  21 us (6%)
    all_gather x4, blocking collectives, gather_in_order(): pieces = lax.all_gather(pieces, axes[k])  92.7 us
    another operation x8, loops' own time, solve_rve(): fluct = lax.fori_loop(0, count, sweep, start)[0]  60.2 us
    reduce_sum x76, other arithmetic, sweep(): step_size = norm_now / jnp.sum(direction * image, axis=(1, 2))  32.2 us
    reduce_sum x76, other arithmetic, sweep(): norm_next = jnp.sum(remain * remain, axis=(1, 2))  18 us
    slice x168, local copies, waits for them, and re-layouts, forward(): return jnp.roll(field, -VOX, axis=-1)  15.4 us
    slice x160, local copies, waits for them, and re-layouts, forward(): jnp.roll(field, VOX - 1, axis=-1)  14.7 us
    slice x168, local copies, waits for them, and re-layouts, forward(): jnp.roll(field, -1, axis=-1)  14.7 us
    add x76, other arithmetic, sweep(): direction = remain + (norm_next / norm_now)[:, None, None] * direction  9.88 us

commit v1 on v0

v1 whole, which is shorter than its diff:
```python
import functools

import jax
import jax.numpy as jnp
import numpy as np
from jax import lax
from jax.experimental import pallas as pl
from jax.experimental.pallas import tpu as pltpu
from jax.sharding import Mesh
from jax.sharding import PartitionSpec as P

VOX = 24
YZ = 576
DEPTH = 8
CELLS = 27
MACRO_ITERS = 8
ROW_COL = ("row_0", "row_1", "col_0", "col_1")
ROW = ("row_0", "row_1")
COL = ("col_0", "col_1")
NEX = 8
NEY = 32
DEVICES = NEX * NEY


def block_order():
    yi, zi, yb, zb = np.meshgrid(np.arange(3), np.arange(3), np.arange(8), np.arange(8), indexing="ij")
    return ((3 * yb + yi) * VOX + 3 * zb + zi).reshape(-1)


def block_matrices():
    order = block_order()
    into = np.zeros((YZ, YZ), np.float32)
    into[order, np.arange(YZ)] = 1.0
    back = np.zeros((640, YZ), np.float32)
    back[np.arange(YZ), order] = 1.0
    return into, back


def at(xi, yi, zi):
    return xi * 9 + yi * 3 + zi


def micro_kernel(
    cond_ref,
    count_ref,
    current_ref,
    load_ref,
    phase_ref,
    grain_ref,
    into_ref,
    back_ref,
    states_ref,
    tangent_ref,
    packed_ref,
    native,
    blocked,
    face,
    edge,
    rhs0,
    res,
    way,
    flu,
    img,
    halo,
    alphas,
    betas,
    norms,
):
    f32 = jnp.float32
    lane = lax.broadcasted_iota(jnp.int32, (8, 128), 1)
    sub = lax.broadcasted_iota(jnp.int32, (8, 128), 0)
    low = lane < 64
    zb = lane & 7
    yb = (lane >> 3) & 7
    z_last, z_first = zb == 7, zb == 0
    y_last, y_first = yb == 7, yb == 0

    def roll(v, shift, axis):
        return pltpu.roll(v, shift, axis)

    ahead = (
        lambda v: roll(v, 7, 0),
        lambda v: jnp.where(y_last, roll(v, 56, 1), roll(v, 120, 1)),
        lambda v: jnp.where(z_last, roll(v, 7, 1), roll(v, 127, 1)),
    )
    before = (
        lambda v: roll(v, 1, 0),
        lambda v: jnp.where(y_first, roll(v, 72, 1), roll(v, 8, 1)),
        lambda v: jnp.where(z_first, roll(v, 121, 1), roll(v, 1, 1)),
    )

    def coords(cell):
        return cell // 9, (cell // 3) % 3, cell % 3

    def side(cell, axis):
        xi, yi, zi = coords(cell)
        return (yi * 3 + zi, xi * 3 + zi, xi * 3 + yi)[axis]

    def moved(cell, axis, step):
        where_at = list(coords(cell))
        where_at[axis] += step
        return at(*where_at)

    def both_halves(acc):
        acc = acc + roll(acc, 4, 0)
        acc = acc + roll(acc, 2, 0)
        acc = acc + roll(acc, 1, 0)
        first = jnp.sum(jnp.where(low, acc, 0.0), axis=1, keepdims=True)
        second = jnp.sum(jnp.where(low, 0.0, acc), axis=1, keepdims=True)
        return first, second

    def total(acc):
        first, second = both_halves(acc)
        return jnp.where(low, first, second)

    phase = phase_ref[...]
    conduct = jnp.where(phase == 0, cond_ref[0], jnp.where(phase == 1, cond_ref[1], cond_ref[2])) * grain_ref[...]
    part_a = conduct.astype(jnp.bfloat16)
    rest = conduct - part_a.astype(f32)
    part_b = rest.astype(jnp.bfloat16)
    part_c = (rest - part_b.astype(f32)).astype(jnp.bfloat16)
    into = into_ref[...]
    ordered = (
        jnp.dot(part_a, into, preferred_element_type=f32)
        + jnp.dot(part_b, into, preferred_element_type=f32)
        + jnp.dot(part_c, into, preferred_element_type=f32)
    )
    for t in range(4):
        native[t] = ordered[:, t * 128 : (t + 1) * 128]
    native[4, :, 0:64] = ordered[:, 512:576]

    for pair in range(4):
        cells = []
        for xi in range(3):
            for g in range(9):
                first = native[g // 2, pl.ds(2 * pair * VOX + xi, 8, stride=3), :]
                second = native[g // 2, pl.ds((2 * pair + 1) * VOX + xi, 8, stride=3), :]
                if g % 2 == 0:
                    cells.append(jnp.where(low, first, roll(second, 64, 1)))
                else:
                    cells.append(jnp.where(low, roll(first, 64, 1), second))
        for axis in range(3):
            faces = []
            for cell in range(CELLS):
                if coords(cell)[axis] < 2:
                    nxt = cells[moved(cell, axis, 1)]
                else:
                    nxt = ahead[axis](cells[moved(cell, axis, -2)])
                faces.append((cells[cell] + nxt) * 0.5)
                face[pair, axis, cell] = faces[cell]
            acc = None
            for cell in range(CELLS):
                if coords(cell)[axis] > 0:
                    back = faces[moved(cell, axis, -1)]
                else:
                    back = before[axis](faces[moved(cell, axis, 2)])
                    edge[pair, axis, side(cell, axis)] = back
                value = faces[cell] - back
                rhs0[pair, axis, cell] = value
                res[pair, axis, cell] = value
                way[pair, axis, cell] = value
                flu[pair, axis, cell] = jnp.zeros((8, 128), f32)
                acc = value * value if acc is None else acc + value * value
            norms[pair, axis] = total(acc)
            alphas[pair, axis] = jnp.zeros((8, 128), f32)
            betas[pair, axis] = jnp.zeros((8, 128), f32)

    def halves_of(pair):
        return jnp.where(low, count_ref[2 * pair], count_ref[2 * pair + 1])

    chains = [(pair, c) for pair in range(4) for c in range(3)]

    def sweep(k, carry):
        for pair, c in chains:
            alpha, beta = alphas[pair, c], betas[pair, c]
            for cell in range(CELLS):
                old = way[pair, c, cell]
                flu[pair, c, cell] = flu[pair, c, cell] + alpha * old
                new = res[pair, c, cell] + beta * old
                way[pair, c, cell] = new
                for axis in range(3):
                    if coords(cell)[axis] == 0:
                        halo[pair, c, 2 * axis, side(cell, axis)] = ahead[axis](new)
                    if coords(cell)[axis] == 2:
                        halo[pair, c, 2 * axis + 1, side(cell, axis)] = before[axis](new)
        for pair, c in chains:
            flow = {}
            acc = None
            for cell in range(CELLS):
                here = way[pair, c, cell]
                out = None
                for axis in range(3):
                    spot = coords(cell)[axis]
                    if spot < 2:
                        nxt = way[pair, c, moved(cell, axis, 1)]
                    else:
                        nxt = halo[pair, c, 2 * axis, side(cell, axis)]
                    flux = face[pair, axis, cell] * (here - nxt)
                    if spot > 0:
                        back = flow.pop((axis, moved(cell, axis, -1)))
                    else:
                        back = edge[pair, axis, side(cell, axis)] * (halo[pair, c, 2 * axis + 1, side(cell, axis)] - here)
                    if spot < 2:
                        flow[axis, cell] = flux
                    out = flux - back if out is None else out + (flux - back)
                img[pair, c, cell] = out
                acc = here * out if acc is None else acc + here * out
            alpha = norms[pair, c] / total(acc)
            alphas[pair, c] = jnp.where(halves_of(pair) > k, alpha, 0.0)
        for pair, c in chains:
            alpha = alphas[pair, c]
            acc = None
            for cell in range(CELLS):
                value = res[pair, c, cell] - alpha * img[pair, c, cell]
                res[pair, c, cell] = value
                acc = value * value if acc is None else acc + value * value
            new = total(acc)
            betas[pair, c] = jnp.where(halves_of(pair) > k, new / norms[pair, c], 0.0)
            norms[pair, c] = new
        return carry

    most = count_ref[0]
    for e in range(1, DEPTH):
        most = jnp.maximum(most, count_ref[e])
    lax.fori_loop(0, most, sweep, 0)

    share = 1.0 / (VOX * YZ)
    packed = jnp.zeros((8, 128), f32)
    tangents = [jnp.zeros((8, 128), f32) for _ in range(DEPTH)]
    for pair in range(4):
        for c in range(3):
            alpha = alphas[pair, c]
            accs = [None] * 3
            for xi in range(3):
                row = []
                for g in range(9):
                    cell = xi * 9 + g
                    value = flu[pair, c, cell] + alpha * way[pair, c, cell]
                    row.append(value)
                    for d in range(3):
                        term = value * rhs0[pair, d, cell]
                        if d == c:
                            term = term - face[pair, d, cell]
                        accs[d] = term if accs[d] is None else accs[d] + term
                start = (2 * pair * 3 + c) * VOX + xi
                for t in range(5):
                    if t < 4:
                        one = jnp.where(low, row[2 * t], roll(row[2 * t + 1], 64, 1))
                        two = jnp.where(low, roll(row[2 * t], 64, 1), row[2 * t + 1])
                    else:
                        one = jnp.where(low, row[8], 0.0)
                        two = jnp.where(low, roll(row[8], 64, 1), 0.0)
                    blocked[t, pl.ds(start, 8, stride=3), :] = one
                    blocked[t, pl.ds(start + 3 * VOX, 8, stride=3), :] = two
            for d in range(3):
                for half, value in enumerate(both_halves(accs[d])):
                    e = 2 * pair + half
                    value = value * (-share)
                    tangents[e] = jnp.where((sub == d) & (lane == c), value, tangents[e])
                    if d == c:
                        packed = jnp.where(lane == d * DEPTH + e, value, packed)
    for e in range(DEPTH):
        tangent_ref[e] = tangents[e][0:3, 0:3]
        packed = jnp.where(lane == 3 * DEPTH + e, current_ref[e], packed)
        packed = jnp.where(lane == 4 * DEPTH + e, load_ref[e], packed)
    for block in range(DEVICES // 8):
        packed_ref[block * 8 : block * 8 + 8, :] = packed

    back = back_ref[...]
    for m in range(3):
        rows = pl.ds(m * 192, 192)
        lhs = jnp.concatenate([blocked[t, rows, :] for t in range(5)], axis=1)
        upper = lhs.astype(jnp.bfloat16)
        lower = (lhs - upper.astype(f32)).astype(jnp.bfloat16)
        states_ref[rows, :] = jnp.dot(upper, back, preferred_element_type=f32) + jnp.dot(
            lower, back, preferred_element_type=f32
        )


def solve_cells(phases, grain, phase_cond, counts, current, load):
    into, back = block_matrices()
    f32 = jnp.float32
    smem = pl.BlockSpec(memory_space=pltpu.SMEM)
    vmem = pl.BlockSpec(memory_space=pltpu.VMEM)
    field = pltpu.VMEM((4, 3, CELLS, 8, 128), f32)
    return pl.pallas_call(
        micro_kernel,
        out_shape=(
            jax.ShapeDtypeStruct((DEPTH * 3 * VOX, YZ), f32),
            jax.ShapeDtypeStruct((DEPTH, 3, 3), f32),
            jax.ShapeDtypeStruct((DEVICES, 128), f32),
        ),
        in_specs=[smem] * 4 + [vmem] * 4,
        out_specs=(vmem, vmem, vmem),
        scratch_shapes=[
            pltpu.VMEM((5, DEPTH * VOX, 128), f32),
            pltpu.VMEM((5, DEPTH * 3 * VOX, 128), f32),
            field,
            pltpu.VMEM((4, 3, 9, 8, 128), f32),
            field,
            field,
            field,
            field,
            field,
            pltpu.VMEM((4, 3, 6, 9, 8, 128), f32),
            pltpu.VMEM((4, 3, 8, 128), f32),
            pltpu.VMEM((4, 3, 8, 128), f32),
            pltpu.VMEM((4, 3, 8, 128), f32),
        ],
        compiler_params=pltpu.CompilerParams(vmem_limit_bytes=40 * 1024 * 1024),
        name="cells",
    )(
        phase_cond,
        counts,
        current,
        load,
        phases,
        grain,
        jnp.asarray(into, jnp.bfloat16),
        jnp.asarray(back, jnp.bfloat16),
    )


def coarse_kernel(place_ref, packed_ref, increment_ref, residual_ref):
    f32 = jnp.float32
    nodes = packed_ref[...].T
    shape = (DEPTH, DEVICES)
    lane = lax.broadcasted_iota(jnp.int32, shape, 1)
    sub = lax.broadcasted_iota(jnp.int32, shape, 0)
    col, row = lane & (NEY - 1), lane >> 5
    has_next = (row < NEX - 1, col < NEY - 1, sub < DEPTH - 1)
    has_back = (row > 0, col > 0, sub > 0)

    def following(v, axis):
        if axis == 2:
            return pltpu.roll(v, DEPTH - 1, 0)
        return pltpu.roll(v, DEVICES - (NEY if axis == 0 else 1), 1)

    def preceding(v, axis):
        if axis == 2:
            return pltpu.roll(v, 1, 0)
        return pltpu.roll(v, NEY if axis == 0 else 1, 1)

    def total(v):
        v = v[:, :128] + v[:, 128:]
        v = v + pltpu.roll(v, 4, 0)
        v = v + pltpu.roll(v, 2, 0)
        v = v + pltpu.roll(v, 1, 0)
        return jnp.sum(v, axis=1, keepdims=True)

    own = None
    links = []
    for axis in range(3):
        k = nodes[axis * DEPTH : (axis + 1) * DEPTH]
        for shift, inside in ((following, has_next[axis]), (preceding, has_back[axis])):
            other = jnp.where(inside, shift(k, axis), 0.0)
            mean = 0.5 * (k + other)
            own = mean if own is None else own + mean
            links.append((shift, axis, jnp.where(inside, mean, 0.0)))

    def apply(v):
        out = own * v
        for shift, axis, weight in links:
            out = out - weight * shift(v, axis)
        return out

    current = nodes[3 * DEPTH : 4 * DEPTH]
    residual = nodes[4 * DEPTH : 5 * DEPTH] - apply(current)
    increment = jnp.zeros(shape, f32)
    direction = residual
    norm_now = total(residual * residual)
    for _ in range(MACRO_ITERS):
        image = apply(direction)
        step = norm_now / total(direction * image)
        increment = increment + step * direction
        residual = residual - step * image
        norm_next = total(residual * residual)
        direction = residual + norm_next / norm_now * direction
        norm_now = norm_next

    spot = sub[:, :128] == lane[:, :128]
    for value, ref in ((increment, increment_ref), (residual, residual_ref)):
        column = jnp.sum(jnp.where(lane == place_ref[0], value, 0.0), axis=1, keepdims=True)
        line = jnp.sum(jnp.where(spot, column, 0.0), axis=0, keepdims=True)
        ref[...] = line[:, :DEPTH]


def solve_coarse(place, packed):
    smem = pl.BlockSpec(memory_space=pltpu.SMEM)
    vmem = pl.BlockSpec(memory_space=pltpu.VMEM)
    line = jax.ShapeDtypeStruct((1, DEPTH), jnp.float32)
    return pl.pallas_call(
        coarse_kernel,
        out_shape=(line, line),
        in_specs=[smem, vmem],
        out_specs=(vmem, vmem),
        name="coarse",
    )(place, packed)


def shards(phases, grain, phase_cond, micro_counts, current, load):
    states, tangent, packed = solve_cells(
        phases.reshape(DEPTH * VOX, YZ),
        grain.reshape(DEPTH * VOX, YZ),
        phase_cond,
        micro_counts.reshape(DEPTH),
        current.reshape(DEPTH),
        load.reshape(DEPTH),
    )
    whole = lax.all_to_all(packed.reshape(DEVICES, 1, 128), ROW_COL, 0, 0, tiled=True)
    place = lax.axis_index(ROW_COL).astype(jnp.int32).reshape(1)
    increment, residual = solve_coarse(place, whole.reshape(DEVICES, 128))
    return (
        states.reshape(1, 1, DEPTH, 3, VOX, YZ),
        tangent.reshape(1, 1, DEPTH, 3, 3),
        increment.reshape(1, 1, DEPTH),
        residual.reshape(1, 1, DEPTH),
    )


def solution(mesh):
    torus = Mesh(mesh.devices.reshape(4, 2, 4, 8), ("row_0", "row_1", "col_0", "col_1"))
    in_specs = (
        P(ROW, COL, None, None, None),
        P(ROW, COL, None, None, None),
        P(),
        P(ROW, COL, None),
        P(ROW, COL, None),
        P(ROW, COL, None),
    )
    out_specs = (
        P(ROW, COL, None, None, None, None),
        P(ROW, COL, None, None, None),
        P(ROW, COL, None),
        P(ROW, COL, None),
    )
    return jax.shard_map(
        shards, mesh=torus, in_specs=in_specs, out_specs=out_specs, check_vma=False
    )
```

time: 327 us -> 63.9 us (0.20); the launches traced: 323 us -> 63.3 us
  blocking collectives: 92.7 us -> 0 us
  other arithmetic: 83.2 us -> 0 us
  loops' own time: 62.4 us -> 0 us
  local copies, waits for them, and re-layouts: 63.7 us -> 8.27 us
  Pallas kernels: 0 us -> 24.1 us
  between operations: 21 us -> 0.67 us
  starting transfers between devices: 0 us -> 17.9 us
  waiting for transfers between devices: 0 us -> 12.3 us
    all_gather x4 -> x0, blocking collectives: 92.7 us -> none  [gather_in_order(): pieces = lax.all_gather(pieces, axes[k])]
    reduce_sum x183 -> x0, other arithmetic: 63.2 us -> none  [the longest x76 32.2 us: sweep(): step_size = norm_now / jnp.sum(direction * image, axis=(1, 2))]
    another operation x9 -> x0, loops' own time: 62.4 us -> none  [the longest x8 60.2 us: solve_rve(): fluct = lax.fori_loop(0, count, sweep, start)[0]]
    slice x763 -> x0, local copies, waits for them, and re-layouts: 52.5 us -> none  [the longest x168 15.4 us: forward(): return jnp.roll(field, -VOX, axis=-1)]
    pallas_call x0 -> x2, Pallas kernels: none -> 24.1 us  [the longest x1 20.4 us: solve_cells(): pl.pallas_call(micro_kernel, out_shape=(jax.ShapeDtypeStruct((DEPTH * 3 *...]
    all_to_all x0 -> x1, starting transfers between devices: none -> 17.9 us  [shards(): lax.all_to_all(packed.reshape(DEVICES, 1, 128), ROW_COL, 0, 0, tiled=True)]
    all_to_all x0 -> x1, waiting for transfers between devices: none -> 12.3 us  [shards(): lax.all_to_all(packed.reshape(DEVICES, 1, 128), ROW_COL, 0, 0, tiled=True)]
    add x82 -> x0, other arithmetic: 9.93 us -> none  [the longest x76 9.88 us: sweep(): direction = remain + (norm_next / norm_now)[:, None, None] * direction]
  transfers between devices with their start and end apart: 0 -> 1, of which waited for: 0 -> 1; matrix products, arithmetic and copies ran while one was open for 0% -> 1% of each run, Pallas kernels for 0% -> 0%
where the time goes in v1:
time: 63.9 us; the launch traced here: 63.3 us
  Pallas kernels  24.1 us (38%)
  starting transfers between devices  17.9 us (28%)
  waiting for transfers between devices  12.3 us (19%)
  local copies, waits for them, and re-layouts  8.27 us (13%)
  between operations  0.67 us (1%)
    pallas_call x1, Pallas kernels, solve_cells(): pl.pallas_call(micro_kernel, out_shape=(jax.ShapeDtypeStruct((DEPTH * 3 *...  20.4 us
    all_to_all x1, starting transfers between devices, shards(): lax.all_to_all(packed.reshape(DEVICES, 1, 128), ROW_COL, 0, 0, tiled=True)  17.9 us
    all_to_all x1, waiting for transfers between devices, shards(): lax.all_to_all(packed.reshape(DEVICES, 1, 128), ROW_COL, 0, 0, tiled=True)  12.3 us
    unnamed x19, local copies, waits for them, and re-layouts  8.27 us
    pallas_call x1, Pallas kernels, solve_coarse(): pl.pallas_call(coarse_kernel, out_shape=(line, line), in_specs=[smem, vme...  3.63 us
  transfers between devices with their start and end apart: 1, of which 1 were waited for; matrix products, arithmetic and copies ran while one was open for 1% of the time, Pallas kernels for 0%

profile of v1, /device:TPU:1, one launch (start us, length us, event | category | flops | bytes accessed | tf_op | source)
XLA Modules:
  0.0 63.3 jit_solution(16250332706232714381)
XLA Ops:
  0.6 0.0 copy-start
  0.6 1.1 %copy-done = bf16[640,576]{1,0:T(8,128)(2,1)S(1)} copy-done((bf16[640,576]{1,0:T(8,128)(2,1)S(1)}, bf16[640,576]{1,0:T(8,128)(2,1)}, u32[]{:S(2)}) %copy-start) | copy-done | bytes 737304
  1.8 0.0 copy-start.1
  1.8 1.1 %copy-done.1 = bf16[576,576]{1,0:T(8,128)(2,1)S(1)} copy-done((bf16[576,576]{1,0:T(8,128)(2,1)S(1)}, bf16[576,576]{1,0:T(8,128)(2,1)}, u32[]{:S(2)}) %copy-start.1) | copy-done | bytes 663576
  2.9 0.0 copy-start.2
  2.9 1.0 %copy-done.2 = s32[1,1,8,24,576]{4,3,2,1,0:T(8,128)S(1)} copy-done((s32[1,1,8,24,576]{4,3,2,1,0:T(8,128)S(1)}, s32[1,1,8,24,576]{4,3,2,1,0:T(8,128)}, u32[]{:S(2)}) %copy-start.2) | copy-done | bytes 442392
  3.9 0.0 copy-start.3
  3.9 1.0 %copy-done.3 = f32[1,1,8,24,576]{4,3,2,1,0:T(8,128)S(1)} copy-done((f32[1,1,8,24,576]{4,3,2,1,0:T(8,128)S(1)}, f32[1,1,8,24,576]{4,3,2,1,0:T(8,128)}, u32[]{:S(2)}) %copy-start.3) | copy-done | bytes 442392
  5.0 0.0 copy-start.4
  5.0 0.7 %copy-done.4 = f32[3]{0:T(128)S(1)} copy-done((f32[3]{0:T(128)S(1)}, f32[3]{0:T(128)}, u32[]{:S(2)}) %copy-start.4) | copy-done | bytes 36
  5.6 0.0 copy-start.5
  5.6 0.7 %copy-done.5 = s32[1,1,8]{2,1,0:T(1,128)S(1)} copy-done((s32[1,1,8]{2,1,0:T(1,128)S(1)}, s32[1,1,8]{2,1,0:T(1,128)}, u32[]{:S(2)}) %copy-start.5) | copy-done | bytes 56
  6.3 0.0 copy-start.6
  6.3 0.7 %copy-done.6 = f32[1,1,8]{2,1,0:T(1,128)S(1)} copy-done((f32[1,1,8]{2,1,0:T(1,128)S(1)}, f32[1,1,8]{2,1,0:T(1,128)}, u32[]{:S(2)}) %copy-start.6) | copy-done | bytes 56
  6.9 0.0 copy-start.7
  6.9 0.7 %copy-done.7 = f32[1,1,8]{2,1,0:T(1,128)S(1)} copy-done((f32[1,1,8]{2,1,0:T(1,128)S(1)}, f32[1,1,8]{2,1,0:T(1,128)}, u32[]{:S(2)}) %copy-start.7) | copy-done | bytes 56
  7.6 20.4 %cells.1 = (f32[576,576]{1,0:T(8,128)}, f32[8,3,3]{2,1,0:T(4,128)S(1)}, f32[256,128]{1,0:T(8,128)}) custom-call(f32[3]{0:T(128)S(1)} %copy-done.4, s32[8]{0:T(128)S(1)} %bitcast.17, f32[8]{0:T(128)S(1)} %bitcast.18, f32[8]{0:T(128)S(1)} %bitcast.19, s32[192,576]{1,0:T(8,128)S(1)} %bitcast.14, f32[192,576]{1,0:T(8,128)S(1)} %bitcast.15, ...), custom_call_target="tpu_custom_call" | custom-call | tf_op jit(solution)/shard_map/cells/pallas_call | solution.py:286
  28.0 17.9 %all-to-all-start = ((f32[256,1,128]{2,1,0:T(1,128)}), f32[256,1,128]{2,1,0:T(1,128)S(1)}, u32[]{:S(2)}, u32[]{:S(2)}) async-start(f32[256,1,128]{2,1,0:T(1,128)} %bitcast.9), calls=%async_computation | async-start | bytes 262144 | tf_op jit(solution)/shard_map/all_to_all | solution.py:410
  46.0 0.7 %copy.16 = f32[1,1,8,3,3]{2,1,4,3,0:T(1,128)} copy(f32[1,1,8,3,3]{4,3,2,1,0:T(4,128)S(1)} %bitcast.16) | data formatting | bytes 576
  46.6 12.3 %all-to-all-done = f32[256,1,128]{2,1,0:T(1,128)S(1)} async-done(((f32[256,1,128]{2,1,0:T(1,128)}), f32[256,1,128]{2,1,0:T(1,128)S(1)}, u32[]{:S(2)}, u32[]{:S(2)}) %all-to-all-start) | async-done | bytes 131104 | tf_op jit(solution)/shard_map/all_to_all | solution.py:410
  59.0 0.0 copy-start.8
  59.0 0.6 %copy-done.8 = f32[256,1,128]{2,1,0:T(1,128)} copy-done((f32[256,1,128]{2,1,0:T(1,128)}, f32[256,1,128]{2,1,0:T(1,128)S(1)}, u32[]{:S(2)}) %copy-start.8) | copy-done | bytes 131096
  59.6 3.6 %coarse.1 = (f32[1,8]{1,0:T(1,128)}, f32[1,8]{1,0:T(1,128)}) custom-call(s32[1]{0:T(128)} %bitcast.7.place_ref, f32[256,128]{1,0:T(8,128)} %bitcast.20), custom_call_target="tpu_custom_call" | custom-call | tf_op jit(solution)/shard_map/coarse/pallas_call | solution.py:392
Async XLA Ops:
  0.6 1.1 %copy-start = (bf16[640,576]{1,0:T(8,128)(2,1)S(1)}, bf16[640,576]{1,0:T(8,128)(2,1)}, u32[]{:S(2)}) copy-start(bf16[640,576]{1,0:T(8,128)(2,1)} %constant.29.clone.back_ref) | copy-start | bytes 2211844
  1.8 1.1 %copy-start.1 = (bf16[576,576]{1,0:T(8,128)(2,1)S(1)}, bf16[576,576]{1,0:T(8,128)(2,1)}, u32[]{:S(2)}) copy-start(bf16[576,576]{1,0:T(8,128)(2,1)} %constant.28.clone.into_ref) | copy-start | bytes 1990660
  2.9 1.0 %copy-start.2 = (s32[1,1,8,24,576]{4,3,2,1,0:T(8,128)S(1)}, s32[1,1,8,24,576]{4,3,2,1,0:T(8,128)}, u32[]{:S(2)}) copy-start(s32[1,1,8,24,576]{4,3,2,1,0:T(8,128)} %param.8) | copy-start | bytes 1327108
  3.9 1.0 %copy-start.3 = (f32[1,1,8,24,576]{4,3,2,1,0:T(8,128)S(1)}, f32[1,1,8,24,576]{4,3,2,1,0:T(8,128)}, u32[]{:S(2)}) copy-start(f32[1,1,8,24,576]{4,3,2,1,0:T(8,128)} %param.9) | copy-start | bytes 1327108
  5.0 0.7 %copy-start.4 = (f32[3]{0:T(128)S(1)}, f32[3]{0:T(128)}, u32[]{:S(2)}) copy-start(f32[3]{0:T(128)} %cond_ref.1) | copy-start | bytes 40
  5.6 0.7 %copy-start.5 = (s32[1,1,8]{2,1,0:T(1,128)S(1)}, s32[1,1,8]{2,1,0:T(1,128)}, u32[]{:S(2)}) copy-start(s32[1,1,8]{2,1,0:T(1,128)} %param.11) | copy-start | bytes 100
  6.3 0.7 %copy-start.6 = (f32[1,1,8]{2,1,0:T(1,128)S(1)}, f32[1,1,8]{2,1,0:T(1,128)}, u32[]{:S(2)}) copy-start(f32[1,1,8]{2,1,0:T(1,128)} %param.12) | copy-start | bytes 100
  6.9 0.7 %copy-start.7 = (f32[1,1,8]{2,1,0:T(1,128)S(1)}, f32[1,1,8]{2,1,0:T(1,128)}, u32[]{:S(2)}) copy-start(f32[1,1,8]{2,1,0:T(1,128)} %param.13) | copy-start | bytes 100
  28.0 31.0 %all-to-all-start = ((f32[256,1,128]{2,1,0:T(1,128)}), f32[256,1,128]{2,1,0:T(1,128)S(1)}, u32[]{:S(2)}, u32[]{:S(2)}) async-start(f32[256,1,128]{2,1,0:T(1,128)} %bitcast.9), calls=%async_computation | async-start | bytes 262144 | tf_op jit(solution)/shard_map/all_to_all | solution.py:410
  59.0 0.7 %copy-start.8 = (f32[256,1,128]{2,1,0:T(1,128)}, f32[256,1,128]{2,1,0:T(1,128)S(1)}, u32[]{:S(2)}) copy-start(f32[256,1,128]{2,1,0:T(1,128)S(1)} %all-to-all-done) | copy-start | bytes 393220

commit v2 on v1

v2 whole, which is shorter than its diff:
```python
import functools

import jax
import jax.numpy as jnp
import numpy as np
from jax import lax
from jax.experimental import pallas as pl
from jax.experimental.pallas import tpu as pltpu
from jax.sharding import Mesh
from jax.sharding import PartitionSpec as P

VOX = 24
YZ = 576
DEPTH = 8
CELLS = 27
MACRO_ITERS = 8
MICRO_MAX = 12
LANE_TAKE = True
MICRO_MIN = 6
VMEM = 67_043_328
EARLY = 8
LEAD = 12
ROW_COL = ("row_0", "row_1", "col_0", "col_1")
ROW = ("row_0", "row_1")
COL = ("col_0", "col_1")
NEX = 8
NEY = 32
DEVICES = NEX * NEY


def block_order():
    yi, zi, yb, zb = np.meshgrid(np.arange(3), np.arange(3), np.arange(8), np.arange(8), indexing="ij")
    return ((3 * yb + yi) * VOX + 3 * zb + zi).reshape(-1)


def block_matrices():
    order = block_order()
    into = np.zeros((YZ, YZ), np.float32)
    into[order, np.arange(YZ)] = 1.0
    back = np.zeros((640, YZ), np.float32)
    back[np.arange(YZ), order] = 1.0
    return into, back


def at(xi, yi, zi):
    return xi * 9 + yi * 3 + zi


def helpers():
    lane = lax.broadcasted_iota(jnp.int32, (8, 128), 1)
    sub = lax.broadcasted_iota(jnp.int32, (8, 128), 0)
    low = lane < 64
    high_part, yb, zb = lane & 64, (lane >> 3) & 7, lane & 7
    y_part, z_part = lane & 56, lane & 7
    y_next = high_part | ((y_part + 8) & 56) | z_part
    y_prev = high_part | ((y_part + 56) & 56) | z_part
    z_next = high_part | y_part | ((z_part + 1) & 7)
    z_prev = high_part | y_part | ((z_part + 7) & 7)

    def taken(v, index):
        return jnp.take_along_axis(v, index, axis=1, mode="promise_in_bounds")

    if LANE_TAKE:
        ahead = (
            lambda v: pltpu.roll(v, 7, 0),
            lambda v: taken(v, y_next),
            lambda v: taken(v, z_next),
        )
        before = (
            lambda v: pltpu.roll(v, 1, 0),
            lambda v: taken(v, y_prev),
            lambda v: taken(v, z_prev),
        )
    else:
        ahead = (
            lambda v: pltpu.roll(v, 7, 0),
            lambda v: jnp.where(yb == 7, pltpu.roll(v, 56, 1), pltpu.roll(v, 120, 1)),
            lambda v: jnp.where(zb == 7, pltpu.roll(v, 7, 1), pltpu.roll(v, 127, 1)),
        )
        before = (
            lambda v: pltpu.roll(v, 1, 0),
            lambda v: jnp.where(yb == 0, pltpu.roll(v, 72, 1), pltpu.roll(v, 8, 1)),
            lambda v: jnp.where(zb == 0, pltpu.roll(v, 121, 1), pltpu.roll(v, 1, 1)),
        )

    def both_halves(acc):
        acc = acc + pltpu.roll(acc, 4, 0)
        acc = acc + pltpu.roll(acc, 2, 0)
        acc = acc + pltpu.roll(acc, 1, 0)
        first = jnp.sum(jnp.where(low, acc, 0.0), axis=1, keepdims=True)
        second = jnp.sum(jnp.where(low, 0.0, acc), axis=1, keepdims=True)
        return first, second

    def total(acc):
        first, second = both_halves(acc)
        return jnp.where(low, first, second)

    return lane, sub, low, ahead, before, both_halves, total


def coords(cell):
    return cell // 9, (cell // 3) % 3, cell % 3


def side(cell, axis):
    xi, yi, zi = coords(cell)
    return (yi * 3 + zi, xi * 3 + zi, xi * 3 + yi)[axis]


def moved(cell, axis, step):
    spot = list(coords(cell))
    spot[axis] += step
    return at(*spot)


def cells_kernel(
    cond_hbm,
    count_hbm,
    current_hbm,
    load_hbm,
    phase_hbm,
    grain_hbm,
    into_hbm,
    path_hbm,
    steps_hbm,
    rhs0_hbm,
    sums_hbm,
    packed_hbm,
    path,
    steps,
    rhs0,
    sums,
    packed_ref,
    cond_ref,
    count_ref,
    current_ref,
    load_ref,
    phase_ref,
    grain_ref,
    into_ref,
    native,
    face,
    res,
    way,
    img,
    halo,
    alphas,
    betas,
    norms,
    energy,
    partial,
    sems,
    path_sems,
):
    f32 = jnp.float32
    copies = [
        pltpu.make_async_copy(src, dst, sems.at[n])
        for n, (src, dst) in enumerate(
            (
                (phase_hbm, phase_ref),
                (grain_hbm, grain_ref),
                (into_hbm, into_ref),
                (cond_hbm, cond_ref),
                (count_hbm, count_ref),
                (current_hbm, current_ref),
                (load_hbm, load_ref),
            )
        )
    ]
    for copy in copies:
        copy.start()
    lane, sub, low, ahead, before, both_halves, total = helpers()
    zero = jnp.zeros((8, 128), f32)
    for copy in copies:
        copy.wait()

    phase = phase_ref[...]
    conduct = jnp.where(phase == 0, cond_ref[0], jnp.where(phase == 1, cond_ref[1], cond_ref[2])) * grain_ref[...]
    part_a = conduct.astype(jnp.bfloat16)
    rest = conduct - part_a.astype(f32)
    part_b = rest.astype(jnp.bfloat16)
    part_c = (rest - part_b.astype(f32)).astype(jnp.bfloat16)
    into = into_ref[...]
    ordered = (
        jnp.dot(part_a, into, preferred_element_type=f32)
        + jnp.dot(part_b, into, preferred_element_type=f32)
        + jnp.dot(part_c, into, preferred_element_type=f32)
    )
    for t in range(4):
        native[t] = ordered[:, t * 128 : (t + 1) * 128]
    native[4, :, 0:64] = ordered[:, 512:576]

    for pair in range(4):
        cells = []
        for xi in range(3):
            for g in range(9):
                first = native[g // 2, pl.ds(2 * pair * VOX + xi, 8, stride=3), :]
                second = native[g // 2, pl.ds((2 * pair + 1) * VOX + xi, 8, stride=3), :]
                if g % 2 == 0:
                    cells.append(jnp.where(low, first, pltpu.roll(second, 64, 1)))
                else:
                    cells.append(jnp.where(low, pltpu.roll(first, 64, 1), second))
        for axis in range(3):
            faces = []
            acc_face = None
            for cell in range(CELLS):
                if coords(cell)[axis] < 2:
                    nxt = cells[moved(cell, axis, 1)]
                else:
                    nxt = ahead[axis](cells[moved(cell, axis, -2)])
                value = (cells[cell] + nxt) * 0.5
                faces.append(value)
                face[pair, axis, cell] = value
                acc_face = value if acc_face is None else acc_face + value
            acc = None
            for cell in range(CELLS):
                if coords(cell)[axis] > 0:
                    back = faces[moved(cell, axis, -1)]
                else:
                    back = before[axis](faces[moved(cell, axis, 2)])
                value = faces[cell] - back
                rhs0[pair, axis, cell] = value
                res[pair, axis, cell] = value
                way[pair, axis, cell] = value
                path[0, pair, axis, cell] = value
                acc = value * value if acc is None else acc + value * value
            norms[pair, axis] = total(acc)
            sums[pair, axis] = total(acc_face)
            energy[pair, axis] = zero

    most = count_ref[0]
    for e in range(1, DEPTH):
        most = jnp.maximum(most, count_ref[e])

    rhs0_copy = pltpu.make_async_copy(rhs0, rhs0_hbm, sems.at[7])
    rhs0_copy.start()
    sums_copy = pltpu.make_async_copy(sums, sums_hbm, sems.at[8])
    sums_copy.start()

    def path_copy(k):
        return pltpu.make_async_copy(path.at[k], path_hbm.at[k], path_sems.at[k])

    path_copy(0).start()
    chains = [(pair, c) for pair in range(4) for c in range(3)]
    late = chains[EARLY:]

    def active(pair, k):
        return jnp.where(low, count_ref[2 * pair], count_ref[2 * pair + 1]) > k

    def set_step(pair, c, k, curve):
        norm = norms[pair, c]
        alpha = jnp.where(active(pair, k), norm / curve, 0.0)
        alphas[pair, c] = alpha
        steps[k, pair, c] = alpha
        energy[pair, c] = energy[pair, c] + alpha * norm

    def far_fluxes(pair, c):
        for axis in range(3):
            for cell in range(CELLS):
                if coords(cell)[axis] == 2:
                    nxt = ahead[axis](way[pair, c, moved(cell, axis, -2)])
                    halo[pair, c, 2 * axis, side(cell, axis)] = face[pair, axis, cell] * (way[pair, c, cell] - nxt)

    def near_fluxes(pair, c):
        for axis in range(3):
            for spot in range(9):
                halo[pair, c, 2 * axis + 1, spot] = before[axis](halo[pair, c, 2 * axis, spot])

    def images(k):
        for pair, c in chains:
            flow = {}
            acc = None
            for cell in range(CELLS):
                here = way[pair, c, cell]
                out = None
                for axis in range(3):
                    spot = coords(cell)[axis]
                    if spot < 2:
                        flux = face[pair, axis, cell] * (here - way[pair, c, moved(cell, axis, 1)])
                    else:
                        flux = halo[pair, c, 2 * axis, side(cell, axis)]
                    if spot > 0:
                        back = flow.pop((axis, moved(cell, axis, -1)))
                    else:
                        back = halo[pair, c, 2 * axis + 1, side(cell, axis)]
                    if spot < 2:
                        flow[axis, cell] = flux
                    out = flux - back if out is None else out + (flux - back)
                img[pair, c, cell] = out
                acc = here * out if acc is None else acc + here * out
            if (pair, c) in late:
                partial[pair, c] = acc
            else:
                set_step(pair, c, k, total(acc))

    def finish(k):
        for pair, c in late:
            set_step(pair, c, k, total(partial[pair, c]))

    for n, chain in enumerate(chains):
        far_fluxes(*chain)
        if n >= LEAD:
            near_fluxes(*chains[n - LEAD])
    for chain in chains[len(chains) - LEAD :]:
        near_fluxes(*chain)
    images(0)

    def sweep(k, carry):
        finish(k - 1)
        for pair, c in chains:
            alpha = alphas[pair, c]
            acc = None
            for cell in range(CELLS):
                value = res[pair, c, cell] - alpha * img[pair, c, cell]
                res[pair, c, cell] = value
                acc = value * value if acc is None else acc + value * value
            new = total(acc)
            betas[pair, c] = jnp.where(active(pair, k), new / norms[pair, c], 0.0)
            norms[pair, c] = new
        for n, (pair, c) in enumerate(chains):
            beta = betas[pair, c]
            for cell in range(CELLS):
                value = res[pair, c, cell] + beta * way[pair, c, cell]
                way[pair, c, cell] = value
                path[k, pair, c, cell] = value
            far_fluxes(pair, c)
            if n >= LEAD:
                near_fluxes(*chains[n - LEAD])
        path_copy(k).start()
        for chain in chains[len(chains) - LEAD :]:
            near_fluxes(*chain)
        images(k)
        return carry

    lax.fori_loop(1, most, sweep, 0)
    finish(most - 1)
    steps_copy = pltpu.make_async_copy(steps, steps_hbm, sems.at[9])
    steps_copy.start()

    share = 1.0 / (VOX * YZ)
    packed = zero
    for pair in range(4):
        for d in range(3):
            value = (sums[pair, d] - energy[pair, d]) * share
            packed = jnp.where(lane == d * DEPTH + 2 * pair, value, packed)
            packed = jnp.where(lane == d * DEPTH + 2 * pair + 1, pltpu.roll(value, 64, 1), packed)
    for e in range(DEPTH):
        packed = jnp.where(lane == 3 * DEPTH + e, current_ref[e], packed)
        packed = jnp.where(lane == 4 * DEPTH + e, load_ref[e], packed)
    for block in range(DEVICES // 8):
        packed_ref[block * 8 : block * 8 + 8, :] = packed
    packed_copy = pltpu.make_async_copy(packed_ref, packed_hbm, sems.at[10])
    packed_copy.start()

    def settle(k, carry):
        path_copy(k).wait()
        return carry

    lax.fori_loop(0, most, settle, 0)
    rhs0_copy.wait()
    sums_copy.wait()
    steps_copy.wait()
    packed_copy.wait()


def output_kernel(
    count_hbm,
    path_hbm,
    steps_hbm,
    rhs0_hbm,
    sums_hbm,
    back_hbm,
    states_hbm,
    tangent_ref,
    count_ref,
    path,
    steps,
    rhs0,
    sums,
    back_ref,
    flu,
    blocked,
    states_ref,
    sems,
    path_sems,
):
    f32 = jnp.float32
    count_copy = pltpu.make_async_copy(count_hbm, count_ref, sems.at[0])
    count_copy.start()
    steps_copy = pltpu.make_async_copy(steps_hbm, steps, sems.at[1])
    steps_copy.start()

    def path_copy(k):
        return pltpu.make_async_copy(path_hbm.at[k], path.at[k], path_sems.at[k])

    for k in range(MICRO_MIN):
        path_copy(k).start()
    copies = [
        pltpu.make_async_copy(rhs0_hbm, rhs0, sems.at[2]),
        pltpu.make_async_copy(sums_hbm, sums, sems.at[3]),
        pltpu.make_async_copy(back_hbm, back_ref, sems.at[4]),
    ]
    lane, sub, low, ahead, before, both_halves, total = helpers()
    count_copy.wait()
    most = count_ref[0]
    for e in range(1, DEPTH):
        most = jnp.maximum(most, count_ref[e])

    def begin(k, carry):
        path_copy(k).start()
        return carry

    lax.fori_loop(MICRO_MIN, most, begin, 0)
    for copy in copies:
        copy.start()
    steps_copy.wait()
    chains = [(pair, c) for pair in range(4) for c in range(3)]
    path_copy(0).wait()
    for pair, c in chains:
        alpha = steps[0, pair, c]
        for cell in range(CELLS):
            flu[pair, c, cell] = alpha * path[0, pair, c, cell]

    def add(k, carry):
        path_copy(k).wait()
        for pair, c in chains:
            alpha = steps[k, pair, c]
            for cell in range(CELLS):
                flu[pair, c, cell] = flu[pair, c, cell] + alpha * path[k, pair, c, cell]
        return carry

    lax.fori_loop(1, most, add, 0)
    for copy in copies:
        copy.wait()

    share = 1.0 / (VOX * YZ)
    row_e = lax.broadcasted_iota(jnp.int32, (16, 128), 1)
    row_d = lax.broadcasted_iota(jnp.int32, (16, 128), 0)
    tangent = jnp.zeros((16, 128), f32)
    for pair in range(4):
        for c in range(3):
            held = [flu[pair, c, cell] for cell in range(CELLS)]
            accs = [None] * 3
            for cell in range(CELLS):
                for d in range(3):
                    term = held[cell] * rhs0[pair, d, cell]
                    accs[d] = term if accs[d] is None else accs[d] + term
            for xi in range(3):
                row = held[xi * 9 : xi * 9 + 9]
                start = (2 * pair * 3 + c) * VOX + xi
                for t in range(5):
                    if t < 4:
                        one = jnp.where(low, row[2 * t], pltpu.roll(row[2 * t + 1], 64, 1))
                        two = jnp.where(low, pltpu.roll(row[2 * t], 64, 1), row[2 * t + 1])
                    else:
                        one = jnp.where(low, row[8], 0.0)
                        two = jnp.where(low, pltpu.roll(row[8], 64, 1), 0.0)
                    blocked[t, pl.ds(start, 8, stride=3), :] = one
                    blocked[t, pl.ds(start + 3 * VOX, 8, stride=3), :] = two
            for d in range(3):
                value = total(accs[d])
                value = (sums[pair, d] - value if d == c else -value) * share
                for half in range(2):
                    flat = value[0:1, 64 * half : 64 * half + 1]
                    tangent = jnp.where((row_d == 3 * d + c) & (row_e == 2 * pair + half), flat, tangent)
    for n in range(9):
        tangent_ref[n] = tangent[n : n + 1, 0:DEPTH]

    back = back_ref[...]
    states_copies = []
    for m in range(3):
        rows = pl.ds(m * 192, 192)
        lhs = jnp.concatenate([blocked[t, rows, :] for t in range(5)], axis=1)
        upper = lhs.astype(jnp.bfloat16)
        lower = (lhs - upper.astype(f32)).astype(jnp.bfloat16)
        states_ref[rows, :] = jnp.dot(upper, back, preferred_element_type=f32) + jnp.dot(
            lower, back, preferred_element_type=f32
        )
        states_copies.append(pltpu.make_async_copy(states_ref.at[rows], states_hbm.at[rows], sems.at[5 + m]))
        states_copies[m].start()
    for copy in states_copies:
        copy.wait()


def solve_cells(phases, grain, phase_cond, counts, current, load):
    into, back = block_matrices()
    f32 = jnp.float32
    hbm = pl.BlockSpec(memory_space=pltpu.HBM)
    vmem = pl.BlockSpec(memory_space=pltpu.VMEM)
    field = pltpu.VMEM((4, 3, CELLS, 8, 128), f32)
    chain = pltpu.VMEM((4, 3, 8, 128), f32)
    path, steps, rhs0, sums, packed = pl.pallas_call(
        cells_kernel,
        out_shape=(
            jax.ShapeDtypeStruct((MICRO_MAX, 4, 3, CELLS, 8, 128), f32),
            jax.ShapeDtypeStruct((MICRO_MAX, 4, 3, 8, 128), f32),
            jax.ShapeDtypeStruct((4, 3, CELLS, 8, 128), f32),
            jax.ShapeDtypeStruct((4, 3, 8, 128), f32),
            jax.ShapeDtypeStruct((DEVICES, 128), f32),
        ),
        in_specs=[hbm] * 7,
        out_specs=(hbm,) * 5,
        scratch_shapes=[
            pltpu.VMEM((MICRO_MAX, 4, 3, CELLS, 8, 128), f32),
            pltpu.VMEM((MICRO_MAX, 4, 3, 8, 128), f32),
            field,
            chain,
            pltpu.VMEM((DEVICES, 128), f32),
            pltpu.SMEM((3,), f32),
            pltpu.SMEM((DEPTH,), jnp.int32),
            pltpu.SMEM((DEPTH,), f32),
            pltpu.SMEM((DEPTH,), f32),
            pltpu.VMEM((DEPTH * VOX, YZ), jnp.int32),
            pltpu.VMEM((DEPTH * VOX, YZ), f32),
            pltpu.VMEM((YZ, YZ), jnp.bfloat16),
            pltpu.VMEM((5, DEPTH * VOX, 128), f32),
            field,
            field,
            field,
            field,
            pltpu.VMEM((4, 3, 6, 9, 8, 128), f32),
            chain,
            chain,
            chain,
            chain,
            chain,
            pltpu.SemaphoreType.DMA((11,)),
            pltpu.SemaphoreType.DMA((MICRO_MAX,)),
        ],
        compiler_params=pltpu.CompilerParams(vmem_limit_bytes=VMEM),
        name="cells",
    )(phase_cond, counts, current, load, phases, grain, jnp.asarray(into, jnp.bfloat16))

    def output():
        return pl.pallas_call(
            output_kernel,
            out_shape=(
                jax.ShapeDtypeStruct((DEPTH * 3 * VOX, YZ), f32),
                jax.ShapeDtypeStruct((9, 1, DEPTH), f32),
            ),
            in_specs=[hbm] * 6,
            out_specs=(hbm, vmem),
            scratch_shapes=[
                pltpu.SMEM((DEPTH,), jnp.int32),
                pltpu.VMEM((MICRO_MAX, 4, 3, CELLS, 8, 128), f32),
                pltpu.VMEM((MICRO_MAX, 4, 3, 8, 128), f32),
                field,
                chain,
                pltpu.VMEM((640, YZ), jnp.bfloat16),
                field,
                pltpu.VMEM((5, DEPTH * 3 * VOX, 128), f32),
                pltpu.VMEM((DEPTH * 3 * VOX, YZ), f32),
                pltpu.SemaphoreType.DMA((8,)),
                pltpu.SemaphoreType.DMA((MICRO_MAX,)),
            ],
            compiler_params=pltpu.CompilerParams(vmem_limit_bytes=VMEM),
            cost_estimate=pl.CostEstimate(flops=400_000_000, bytes_accessed=4_000_000, transcendentals=0),
            name="output",
        )(counts, path, steps, rhs0, sums, jnp.asarray(back, jnp.bfloat16))

    return packed, output


def coarse_kernel(place_ref, packed_ref, increment_ref, residual_ref):
    f32 = jnp.float32
    nodes = packed_ref[...].T
    shape = (DEPTH, DEVICES)
    lane = lax.broadcasted_iota(jnp.int32, shape, 1)
    sub = lax.broadcasted_iota(jnp.int32, shape, 0)
    col, row = lane & (NEY - 1), lane >> 5
    has_next = (row < NEX - 1, col < NEY - 1, sub < DEPTH - 1)
    has_back = (row > 0, col > 0, sub > 0)

    def following(v, axis):
        if axis == 2:
            return pltpu.roll(v, DEPTH - 1, 0)
        return pltpu.roll(v, DEVICES - (NEY if axis == 0 else 1), 1)

    def preceding(v, axis):
        if axis == 2:
            return pltpu.roll(v, 1, 0)
        return pltpu.roll(v, NEY if axis == 0 else 1, 1)

    def total(v):
        v = v[:, :128] + v[:, 128:]
        v = v + pltpu.roll(v, 4, 0)
        v = v + pltpu.roll(v, 2, 0)
        v = v + pltpu.roll(v, 1, 0)
        return jnp.sum(v, axis=1, keepdims=True)

    own = None
    links = []
    for axis in range(3):
        k = nodes[axis * DEPTH : (axis + 1) * DEPTH]
        for shift, inside in ((following, has_next[axis]), (preceding, has_back[axis])):
            other = jnp.where(inside, shift(k, axis), 0.0)
            mean = 0.5 * (k + other)
            own = mean if own is None else own + mean
            links.append((shift, axis, jnp.where(inside, mean, 0.0)))

    def apply(v):
        out = own * v
        for shift, axis, weight in links:
            out = out - weight * shift(v, axis)
        return out

    current = nodes[3 * DEPTH : 4 * DEPTH]
    residual = nodes[4 * DEPTH : 5 * DEPTH] - apply(current)
    increment = jnp.zeros(shape, f32)
    direction = residual
    norm_now = total(residual * residual)
    for _ in range(MACRO_ITERS):
        image = apply(direction)
        step = norm_now / total(direction * image)
        increment = increment + step * direction
        residual = residual - step * image
        norm_next = total(residual * residual)
        direction = residual + norm_next / norm_now * direction
        norm_now = norm_next

    spot = sub[:, :128] == lane[:, :128]
    for value, ref in ((increment, increment_ref), (residual, residual_ref)):
        column = jnp.sum(jnp.where(lane == place_ref[0], value, 0.0), axis=1, keepdims=True)
        line = jnp.sum(jnp.where(spot, column, 0.0), axis=0, keepdims=True)
        ref[...] = line[:, :DEPTH]


def solve_coarse(place, packed):
    smem = pl.BlockSpec(memory_space=pltpu.SMEM)
    vmem = pl.BlockSpec(memory_space=pltpu.VMEM)
    line = jax.ShapeDtypeStruct((1, DEPTH), jnp.float32)
    return pl.pallas_call(
        coarse_kernel,
        out_shape=(line, line),
        in_specs=[smem, vmem],
        out_specs=(vmem, vmem),
        compiler_params=pltpu.CompilerParams(vmem_limit_bytes=4 * 1024 * 1024),
        name="coarse",
    )(place, packed)


def shards(phases, grain, phase_cond, micro_counts, current, load):
    packed, output = solve_cells(
        phases.reshape(DEPTH * VOX, YZ),
        grain.reshape(DEPTH * VOX, YZ),
        phase_cond,
        micro_counts.reshape(DEPTH),
        current.reshape(DEPTH),
        load.reshape(DEPTH),
    )
    whole = lax.all_to_all(packed.reshape(DEVICES, 1, 128), ROW_COL, 0, 0, tiled=True)
    states, tangent = output()
    place = lax.axis_index(ROW_COL).astype(jnp.int32).reshape(1)
    increment, residual = solve_coarse(place, whole.reshape(DEVICES, 128))
    return (
        states.reshape(1, 1, DEPTH, 3, VOX, YZ),
        tangent.reshape(3, 3, 1, 1, DEPTH).transpose(2, 3, 4, 0, 1),
        increment.reshape(1, 1, DEPTH),
        residual.reshape(1, 1, DEPTH),
    )


def solution(mesh):
    torus = Mesh(mesh.devices.reshape(4, 2, 4, 8), ("row_0", "row_1", "col_0", "col_1"))
    in_specs = (
        P(ROW, COL, None, None, None),
        P(ROW, COL, None, None, None),
        P(),
        P(ROW, COL, None),
        P(ROW, COL, None),
        P(ROW, COL, None),
    )
    out_specs = (
        P(ROW, COL, None, None, None, None),
        P(ROW, COL, None, None, None),
        P(ROW, COL, None),
        P(ROW, COL, None),
    )
    return jax.shard_map(
        shards, mesh=torus, in_specs=in_specs, out_specs=out_specs, check_vma=False
    )
```

time: 63.9 us -> 53 us (0.83); the launches traced: 63.3 us -> 53 us
  waiting for transfers between devices: 12.3 us -> 3.69 us
  local copies, waits for them, and re-layouts: 8.27 us -> 0 us
  starting transfers between devices: 17.9 us -> 23 us
  Pallas kernels: 24.1 us -> 25.6 us
    all_to_all x1, waiting for transfers between devices: 12.3 us -> 3.69 us  [shards(): lax.all_to_all(packed.reshape(DEVICES, 1, 128), ROW_COL, 0, 0, tiled=True)]
    unnamed x19 -> x0, local copies, waits for them, and re-layouts: 8.27 us -> none
    all_to_all x1, starting transfers between devices: 17.9 us -> 23 us  [shards(): lax.all_to_all(packed.reshape(DEVICES, 1, 128), ROW_COL, 0, 0, tiled=True)]
    pallas_call x1 -> x2, Pallas kernels: 20.4 us -> 22 us  [the longest x1 13 us: solve_cells(): pl.pallas_call(cells_kernel, out_shape=(jax.ShapeDtypeStruct((MICRO_MAX,...]
  transfers between devices with their start and end apart: 1 -> 1, of which waited for: 1 -> 1; matrix products, arithmetic and copies ran while one was open for 1% -> 0% of each run, Pallas kernels for 0% -> 17%
where the time goes in v2:
time: 53 us
  Pallas kernels  25.6 us (48%)
  starting transfers between devices  23 us (43%)
  waiting for transfers between devices  3.69 us (7%)
  between operations  0.67 us (1%)
    all_to_all x1, starting transfers between devices, shards(): lax.all_to_all(packed.reshape(DEVICES, 1, 128), ROW_COL, 0, 0, tiled=True)  23 us
    pallas_call x1, Pallas kernels, solve_cells(): pl.pallas_call(cells_kernel, out_shape=(jax.ShapeDtypeStruct((MICRO_MAX,...  13 us
    pallas_call x1, Pallas kernels, output(): pl.pallas_call(output_kernel, out_shape=(jax.ShapeDtypeStruct((DEPTH * 3...  8.97 us
    all_to_all x1, waiting for transfers between devices, shards(): lax.all_to_all(packed.reshape(DEVICES, 1, 128), ROW_COL, 0, 0, tiled=True)  3.69 us
    pallas_call x1, Pallas kernels, solve_coarse(): pl.pallas_call(coarse_kernel, out_shape=(line, line), in_specs=[smem, vme...  3.63 us
  transfers between devices with their start and end apart: 1, of which 1 were waited for; matrix products, arithmetic and copies ran while one was open for 0% of the time, Pallas kernels for 17%

profile of v2, /device:TPU:1, one launch (start us, length us, event | category | flops | bytes accessed | tf_op | source)
XLA Modules:
  0.0 53.0 jit_solution(7982463441621265123)
XLA Ops:
  0.6 13.0 %cells.1 = (f32[12,4,3,27,8,128]{5,4,3,2,1,0:T(8,128)}, f32[12,4,3,8,128]{4,3,2,1,0:T(8,128)}, f32[4,3,27,8,128]{4,3,2,1,0:T(8,128)}, f32[4,3,8,128]{3,2,1,0:T(8,128)}, f32[256,128]{1,0:T(8,128)}) custom-call(f32[3]{0:T(128)} %cond_hbm.1, s32[8]{0:T(128)} %bitcast.21, f32[8]{0:T(128)} %bitcast.23, f32[8]{0:T(128)} %bitcast.24, s32[192,576]{1,0:T(8,128)} %bitcast.18, ...), custom_call_target="tpu_custom_call" | custom-call | tf_op jit(solution)/shard_map/cells/pallas_call | solution.py:492
  13.7 23.0 %all-to-all-start = ((f32[256,1,128]{2,1,0:T(1,128)}), f32[256,1,128]{2,1,0:T(1,128)}, u32[]{:S(2)}, u32[]{:S(2)}) async-start(f32[256,1,128]{2,1,0:T(1,128)} %bitcast.20), calls=%async_computation | async-start | bytes 262144 | tf_op jit(solution)/shard_map/all_to_all | solution.py:651
  36.7 9.0 %output.1 = (f32[576,576]{1,0:T(8,128)}, f32[9,1,8]{2,1,0:T(1,128)}) custom-call(s32[8]{0:T(128)} %bitcast.22, f32[12,4,3,27,8,128]{5,4,3,2,1,0:T(8,128)} %get-tuple-element.13.path_hbm, f32[12,4,3,8,128]{4,3,2,1,0:T(8,128)} %get-tuple-element.14.steps_hbm, f32[4,3,27,8,128]{4,3,2,1,0:T(8,128)} %get-tuple-element.15.rhs0_hbm, ...), custom_call_target="tpu_custom_call" | custom-call | flops 400000000 | bytes 4000000 | tf_op jit(solution)/shard_map/output/pallas_call | solution.py:535
  45.7 3.7 %all-to-all-done = f32[256,1,128]{2,1,0:T(1,128)} async-done(((f32[256,1,128]{2,1,0:T(1,128)}), f32[256,1,128]{2,1,0:T(1,128)}, u32[]{:S(2)}, u32[]{:S(2)}) %all-to-all-start) | async-done | bytes 131104 | tf_op jit(solution)/shard_map/all_to_all | solution.py:651
  49.4 3.6 %coarse.1 = (f32[1,8]{1,0:T(1,128)}, f32[1,8]{1,0:T(1,128)}) custom-call(s32[1]{0:T(128)} %bitcast.9.place_ref, f32[256,128]{1,0:T(8,128)} %bitcast.12.packed_ref), custom_call_target="tpu_custom_call" | custom-call | tf_op jit(solution)/shard_map/coarse/pallas_call | solution.py:632
Async XLA Ops:
  13.7 35.7 %all-to-all-start = ((f32[256,1,128]{2,1,0:T(1,128)}), f32[256,1,128]{2,1,0:T(1,128)}, u32[]{:S(2)}, u32[]{:S(2)}) async-start(f32[256,1,128]{2,1,0:T(1,128)} %bitcast.20), calls=%async_computation | async-start | bytes 262144 | tf_op jit(solution)/shard_map/all_to_all | solution.py:651
